TPU v7x, 32 devices: a whole 2x2x4 slice. The times are simulated.
32 devices in a mesh: dm: 4 (over z), tm: 8 (over y, x, core).
Axes of the slice: x: 2, y: 2, z: 4, core: 2. Of those that a mesh axis runs over, the one named last changes fastest.
Arguments:
- dispersed: float32 [1024, 8192], P('dm', 'tm')
- widths: int32 [4], replicated, may hold values from 1 to 129, as said below
Outputs:
- snr: bfloat16 [4, 1024, 8192], P(None, 'dm', 'tm')
- peaks: float32 [4, 1024], P(None, 'dm')
Inputs may be any that keep to these rules, and one draw needn't show every extreme that they name: `widths`: at least one width equals 129.
All inputs are finite; a program needn't handle non-finite values.
Results may differ from a plain program's by a relative error of at most 0.001.
Values sent between devices are 32-bit elements; how exact they have to be, the bound alone decides.
A program may use at most 64 MiB of HBM per device.

v0:
```python
import jax
import jax.numpy as jnp
from jax import lax
from jax.sharding import PartitionSpec as P

HALF = 128
eps_value = 1e-06


def with_halo(x, sides, width):
    for axis, dim in sides:
        peers, length = (lax.axis_size(axis), x.shape[dim])
        up = [(i, (i + 1) % peers) for i in range(peers - 1)]
        down = [(j, i) for i, j in up]
        last = lax.slice_in_dim(x, length - width, length, axis=dim)
        leading = lax.slice_in_dim(x, 0, width, axis=dim)
        before = lax.ppermute(last, axis, up)
        after = lax.ppermute(leading, axis, down)
        x = jnp.concatenate([before, x, after], axis=dim)
    return x


def from_behind(block, axis, distance):
    devices = range(lax.axis_size(axis))
    route = [(i - distance, i) for i in devices if i - distance in devices]
    return lax.ppermute(block, axis, route)


def band_table(span_list, block_len):
    column_idx = jnp.arange(span_list.shape[0] * block_len, dtype=jnp.int32)
    offsets = column_idx % block_len
    reaches = jnp.repeat(span_list, block_len)
    row_idx = jnp.arange(2 * block_len, dtype=jnp.int32)[:, None]
    inside = (row_idx >= offsets[None, :]) & (row_idx < offsets[None, :] + reaches[None, :])
    return inside.astype(jnp.float32)


def window_sum(extended, length, band_matrix, block_len):
    row_count = extended.shape[0]
    block_count = length // block_len
    blocks = extended.reshape(row_count, block_count + 1, block_len)
    paired = jnp.concatenate([blocks[:, :-1], blocks[:, 1:]], axis=2)
    return jnp.einsum("rbs,sk->rbk", paired, band_matrix, precision=lax.Precision.HIGHEST)


def boxcar(extended, length, band_matrix, inverse, block_len):
    row_count = extended.shape[0]
    moving = window_sum(extended, length, band_matrix, block_len)
    moving = moving.reshape(row_count, length // block_len, inverse.shape[0], block_len)
    moving = jnp.transpose(moving, (2, 0, 1, 3)).reshape(inverse.shape[0], row_count, length)
    return moving * inverse[:, None, None]


def body(dispersed, widths):
    row_count, length = dispersed.shape
    block_len = 2 * HALF
    total_len = length * lax.axis_size("tm")
    offset = lax.axis_index("tm") * length
    ma_band = band_table(jnp.full((1,), 2 * HALF + 1, jnp.int32), block_len)
    box_band = band_table(widths, block_len)
    inverse = 1.0 / jnp.sqrt(widths.astype(jnp.float32))

    def counts_at(first_pos, size_len):
        positions = first_pos + jnp.arange(size_len, dtype=jnp.int32)
        counts = (
            jnp.minimum(positions + HALF, total_len - 1) - jnp.maximum(positions - HALF, 0) + 1
        ).astype(jnp.float32)
        inside = (positions >= 0) & (positions < total_len)
        return (counts, inside)

    local_counts = counts_at(offset, length)[0]
    extended = with_halo(dispersed, (("tm", 1),), 2 * HALF)
    wide_counts, inside = counts_at(offset - HALF, length + block_len)
    first_mean = window_sum(extended, length + block_len, ma_band, block_len).reshape(
        row_count, length + block_len
    )
    widened = jnp.where(inside[None, :], first_mean / wide_counts, 0.0)
    smooth_mean = (
        window_sum(widened, length, ma_band, block_len).reshape(row_count, length) / local_counts
    )
    detrended = dispersed - smooth_mean
    padding = jnp.zeros((row_count, HALF), jnp.float32)
    power_sum = lax.psum(jnp.sum(detrended * detrended, axis=1), "tm")
    row_spread_scale = jnp.sqrt(power_sum / total_len + eps_value)
    normed = detrended / row_spread_scale[:, None]
    colsum = lax.psum(jnp.sum(normed, axis=0), "dm")
    cleaned = normed - (colsum / (row_count * lax.axis_size("dm")))[None, :]
    head_cols = from_behind(cleaned[:, :HALF], "tm", -1)
    series = boxcar(
        jnp.concatenate([cleaned, head_cols, padding], axis=1), length, box_band, inverse, block_len
    )
    peak_values = lax.pmax(jnp.max(series, axis=2), "tm")
    return (series.astype(jnp.bfloat16), peak_values)


def solution(mesh):
    placed = (P("dm", "tm"), P())
    return jax.shard_map(
        body,
        mesh=mesh,
        in_specs=placed,
        out_specs=(P(None, "dm", "tm"), P(None, "dm")),
        check_vma=False,
    )
```

profile of v0, /device:TPU:4, one launch (start us, length us, event | category | flops | bytes accessed | tf_op | source)
XLA Modules:
  0.0 113.8 jit_solution(7534095986708861592)
XLA Ops:
  0.6 1.6 %copy.23 = f32[256,1024]{0,1:T(8,128)S(1)} copy(f32[256,1024]{1,0:T(8,128)} %param.2) | data formatting | bytes 2097152 | tf_op args[0]
  2.3 1.9 %collective-permute-start = (f32[256,256]{0,1:T(8,128)S(1)}, f32[256,256]{0,1:T(8,128)S(1)}, u32[]{:S(2)}, u32[]{:S(2)}) collective-permute-start(f32[256,256]{0,1:T(8,128)S(1)} %get-tuple-element.12), channel_id=1, source_target_pairs={{0,1},{1,2},{2,3},{3,4},{4,5},{5,6},{6,7},{8,9},{9,10},{10,11},{11... | collective-permute-start | bytes 786440 | tf_op jit(solution)/shard_map/ppermute | solution.py:17
  4.2 4.5 %collective-permute-start.1 = (f32[256,256]{0,1:T(8,128)S(1)}, f32[256,256]{0,1:T(8,128)S(1)}, u32[]{:S(2)}, u32[]{:S(2)}) collective-permute-start(f32[256,256]{0,1:T(8,128)S(1)} %get-tuple-element.13), channel_id=1, source_target_pairs={{1,0},{2,1},{3,2},{4,3},{5,4},{6,5},{7,6},{9,8},{10,9},{11,10},{12... | collective-permute-start | bytes 786440 | tf_op jit(solution)/shard_map/ppermute | solution.py:18
  8.9 2.0 %collective-permute-done = f32[256,256]{0,1:T(8,128)S(1)} collective-permute-done((f32[256,256]{0,1:T(8,128)S(1)}, f32[256,256]{0,1:T(8,128)S(1)}, u32[]{:S(2)}, u32[]{:S(2)}) %collective-permute-start) | collective-permute-done | bytes 262176 | tf_op jit(solution)/shard_map/ppermute | solution.py:17
  10.9 1.7 %collective-permute-done.1 = f32[256,256]{0,1:T(8,128)S(1)} collective-permute-done((f32[256,256]{0,1:T(8,128)S(1)}, f32[256,256]{0,1:T(8,128)S(1)}, u32[]{:S(2)}, u32[]{:S(2)}) %collective-permute-start.1) | collective-permute-done | bytes 262176 | tf_op jit(solution)/shard_map/ppermute | solution.py:18
  12.7 1.3 %fusion.40 = (f32[256,5,256]{0,2,1:T(8,128)}, f32[256,5,256]{0,2,1:T(8,128)S(1)}) fusion(f32[256,6,256]{0,2,1:T(8,128)S(1)} %bitcast.22), kind=kLoop, calls=%fused_computation.58 | loop fusion | bytes 5242880 | tf_op jit(solution)/shard_map/slice | solution.py:42
  14.0 2.8 %copy.29 = f32[256,5,256]{2,0,1:T(8,128)} copy(f32[256,5,256]{0,2,1:T(8,128)} %get-tuple-element.6) | data formatting | bytes 2621440
  16.8 1.5 %copy.30 = f32[256,5,256]{2,0,1:T(8,128)} copy(f32[256,5,256]{0,2,1:T(8,128)S(1)} %get-tuple-element.7) | data formatting | bytes 2621440
  18.2 3.4 %divide_select_fusion = f32[256,5,256]{0,2,1:T(8,128)S(1)} fusion(f32[256,5,256]{2,0,1:T(8,128)} %copy.30, f32[256,5,256]{2,0,1:T(8,128)} %copy.29, f32[5,256]{1,0:T(8,128)S(1)} %add_convert_fusion, pred[5,256]{1,0:T(8,128)(4,1)S(1)} %fusion.31, s32[256]{0:T(256)S(1)} %get-tuple-element.15, s32[256]{0:T(256)S(1)} %get-tuple-element.14), kind=kOutput, calls=%fused_computation.20 | convolution fusion | flops 2014969856 | bytes 3940608 | tf_op jit(solution)/shard_map/rbs,sk->rbk/dot_general | solution.py:43
  21.8 1.3 %fusion.4 = f32[256,4,256]{0,2,1:T(8,128)S(1)} fusion(f32[256,4,256]{0,2,1:T(8,128)S(1)} %get-tuple-element.11, f32[256,4,256]{0,2,1:T(8,128)S(1)} %get-tuple-element.10, s32[256]{0:T(256)S(1)} %get-tuple-element.15, s32[256]{0:T(256)S(1)} %get-tuple-element.14), kind=kOutput, calls=%fused_computation.6 | convolution fusion | flops 1611530240 | bytes 3147776 | tf_op jit(solution)/shard_map/rbs,sk->rbk/dot_general | solution.py:43
  23.4 14.6 %psum.14 = f32[256]{0:T(256)S(1)} all-reduce(f32[256]{0:T(256)S(1)} %get-tuple-element.4), channel_id=1, replica_groups=mesh['dm'=4,'tm'=8] {'tm'}, use_global_device_ids=true, to_apply=%region_1.2 | all-reduce | flops 256 | bytes 2048 | tf_op jit(solution)/shard_map/psum | solution.py:83
  38.2 12.0 %psum.15 = f32[1024]{0:T(1024)S(1)} all-reduce(f32[1024]{0:T(1024)S(1)} %fusion.22), channel_id=1, replica_groups=mesh['dm'=4,'tm'=8] {'dm'}, use_global_device_ids=true, to_apply=%region_3.4 | all-reduce | flops 1024 | bytes 8192 | tf_op jit(solution)/shard_map/psum | solution.py:86
  50.4 1.9 %collective-permute-start.2 = (f32[256,128]{0,1:T(8,128)S(1)}, f32[256,128]{0,1:T(8,128)S(1)}, u32[]{:S(2)}, u32[]{:S(2)}) collective-permute-start(f32[256,128]{0,1:T(8,128)S(1)} %slice.42), channel_id=1, source_target_pairs={{1,0},{2,1},{3,2},{4,3},{5,4},{6,5},{7,6},{9,8},{10,9},{11,10},{12... | collective-permute-start | bytes 393224 | tf_op jit(solution)/shard_map/ppermute | solution.py:26
  52.4 2.5 %collective-permute-done.2 = f32[256,128]{0,1:T(8,128)S(1)} collective-permute-done((f32[256,128]{0,1:T(8,128)S(1)}, f32[256,128]{0,1:T(8,128)S(1)}, u32[]{:S(2)}, u32[]{:S(2)}) %collective-permute-start.2) | collective-permute-done | bytes 131104 | tf_op jit(solution)/shard_map/ppermute | solution.py:26
  55.3 0.3 copy.31
  55.6 0.3 copy.32
  56.0 5.2 %fusion.8 = f32[256,4,1024]{2,0,1:T(8,128)} fusion(f32[256,4,256]{2,0,1:T(8,128)S(1)} %copy.32, f32[256,4,256]{2,0,1:T(8,128)S(1)} %copy.31, s32[1024]{0:T(1024)S(1)} %get-tuple-element.17, s32[1024]{0:T(1024)S(1)} %get-tuple-element.16), kind=kOutput, calls=%fused_computation.10 | convolution fusion | flops 6444548096 | bytes 6299648 | tf_op jit(solution)/shard_map/rbs,sk->rbk/dot_general | solution.py:43
  61.2 5.6 %reshape.95 = f32[256,4,4,256]{3,2,0,1:T(4,128)} reshape(f32[256,4,1024]{2,0,1:T(8,128)} %fusion.8) | data formatting | bytes 8388608 | tf_op jit(solution)/shard_map/reshape | solution.py:49
  66.8 3.2 %multiply_reduce_fusion = f32[4,256]{0,1:T(8,128)S(1)} fusion(f32[4]{0:T(128)S(1)} %convert_rsqrt_fusion, f32[256,4,4,256]{3,2,0,1:T(4,128)} %reshape.95), kind=kLoop, calls=%fused_computation | loop fusion | flops 2096128 | bytes 4198416 | tf_op jit(solution)/shard_map/reduce_max | solution.py:92
  70.0 26.4 %pmax.7 = f32[4,256]{0,1:T(8,128)S(1)} all-reduce(f32[4,256]{0,1:T(8,128)S(1)} %multiply_reduce_fusion), channel_id=1, replica_groups=mesh['dm'=4,'tm'=8] {'tm'}, use_global_device_ids=true, to_apply=%region_5.6 | all-reduce | flops 1024 | bytes 8192 | tf_op jit(solution)/shard_map/pmax | solution.py:92
  96.4 0.7 copy.27
  97.0 6.9 %copy.26 = f32[4,256,4,256]{3,2,1,0:T(4,128)} copy(f32[4,256,4,256]{3,0,1,2:T(4,128)} %bitcast.21) | data formatting | bytes 8388608 | tf_op jit(solution)/shard_map/transpose | solution.py:50
  103.9 5.8 %reshape.96 = f32[4,256,1024]{2,1,0:T(8,128)} reshape(f32[4,256,4,256]{3,2,1,0:T(4,128)} %copy.26) | data formatting | bytes 8388608 | tf_op jit(solution)/shard_map/reshape | solution.py:50
  109.7 4.1 %multiply_convert_fusion = bf16[4,256,1024]{2,1,0:T(8,128)(2,1)} fusion(f32[4,256,1024]{2,1,0:T(8,128)} %reshape.96, f32[4]{0:T(128)S(1)} %convert_rsqrt_fusion), kind=kLoop, calls=%fused_computation.1 | loop fusion | flops 2097152 | bytes 6291472 | tf_op jit(solution)/shard_map/convert_element_type | solution.py:93
  (23 shorter events, 1.6 us)
Async XLA Ops:
  0.6 8.2 %copy-start = (s32[4]{0:T(128)S(1)}, s32[4]{0:T(128)}, u32[]{:S(2)}) copy-start(s32[4]{0:T(128)} %param.3) | copy-start | bytes 52
  2.3 8.7 %collective-permute-start = (f32[256,256]{0,1:T(8,128)S(1)}, f32[256,256]{0,1:T(8,128)S(1)}, u32[]{:S(2)}, u32[]{:S(2)}) collective-permute-start(f32[256,256]{0,1:T(8,128)S(1)} %get-tuple-element.12), channel_id=1, source_target_pairs={{0,1},{1,2},{2,3},{3,4},{4,5},{5,6},{6,7},{8,9},{9,10},{10,11},{11... | collective-permute-start | bytes 786440 | tf_op jit(solution)/shard_map/ppermute | solution.py:17
  4.2 8.4 %collective-permute-start.1 = (f32[256,256]{0,1:T(8,128)S(1)}, f32[256,256]{0,1:T(8,128)S(1)}, u32[]{:S(2)}, u32[]{:S(2)}) collective-permute-start(f32[256,256]{0,1:T(8,128)S(1)} %get-tuple-element.13), channel_id=1, source_target_pairs={{1,0},{2,1},{3,2},{4,3},{5,4},{6,5},{7,6},{9,8},{10,9},{11,10},{12... | collective-permute-start | bytes 786440 | tf_op jit(solution)/shard_map/ppermute | solution.py:18
  50.4 4.4 %collective-permute-start.2 = (f32[256,128]{0,1:T(8,128)S(1)}, f32[256,128]{0,1:T(8,128)S(1)}, u32[]{:S(2)}, u32[]{:S(2)}) collective-permute-start(f32[256,128]{0,1:T(8,128)S(1)} %slice.42), channel_id=1, source_target_pairs={{1,0},{2,1},{3,2},{4,3},{5,4},{6,5},{7,6},{9,8},{10,9},{11,10},{12... | collective-permute-start | bytes 393224 | tf_op jit(solution)/shard_map/ppermute | solution.py:26
where the time goes:
time: 114 us
  blocking collectives  53 us (46%)
  local copies, waits for them, and re-layouts  27.2 us (24%)
  matrix products  9.89 us (9%)
  other arithmetic  8.4 us (7%)
  starting transfers between devices  8.38 us (7%)
  waiting for transfers between devices  6.19 us (5%)
    pmax x1, blocking collectives, body(): peak_values = lax.pmax(jnp.max(series, axis=2), 'tm')  26.4 us
    psum x1, blocking collectives, body(): power_sum = lax.psum(jnp.sum(detrended * detrended, axis=1), 'tm')  14.6 us
    psum x1, blocking collectives, body(): colsum = lax.psum(jnp.sum(normed, axis=0), 'dm')  12 us
    dot_general x3, matrix products, window_sum(): jnp.einsum('rbs,sk->rbk', paired, band_matrix, precision=lax.Precision.HI...  9.89 us
    unnamed x10, local copies, waits for them, and re-layouts  7.21 us
    transpose x1, local copies, waits for them, and re-layouts, boxcar(): jnp.transpose(moving, (2, 0, 1, 3))  6.85 us
    reshape x1, local copies, waits for them, and re-layouts, boxcar(): jnp.transpose(moving, (2, 0, 1, 3))  5.78 us
    reshape x1, local copies, waits for them, and re-layouts, boxcar(): moving.reshape(row_count, length // block_len, inverse.shape[0], block_len)  5.62 us
  transfers between devices with their start and end apart: 3, of which 3 were waited for; matrix products, arithmetic and copies ran while one was open for 0% of the time, Pallas kernels for 0%

commit v1 on v0

--- a/solution.py
+++ b/solution.py
@@ -80,7 +80,7 @@
     )
     detrended = dispersed - smooth_mean
     padding = jnp.zeros((row_count, HALF), jnp.float32)
-    power_sum = lax.psum(jnp.sum(detrended * detrended, axis=1), "tm")
+    power_sum = jnp.sum(lax.all_gather(jnp.sum(detrended * detrended, axis=1), "tm"), axis=0)
     row_spread_scale = jnp.sqrt(power_sum / total_len + eps_value)
     normed = detrended / row_spread_scale[:, None]
     colsum = lax.psum(jnp.sum(normed, axis=0), "dm")

time: 114 us -> 109 us (0.956)
  blocking collectives: 53 us -> 47.5 us
    psum x1 -> x0, blocking collectives: 14.6 us -> none  [body(): power_sum = lax.psum(jnp.sum(detrended * detrended, axis=1), 'tm')]
    all_gather x0 -> x1, blocking collectives: none -> 9.15 us  [body(): lax.all_gather(jnp.sum(detrended * detrended, axis=1), 'tm')]
where the time goes in v1:
time: 109 us; the launch traced here: 108 us
  blocking collectives  47.5 us (44%)
  local copies, waits for them, and re-layouts  27.2 us (25%)
  matrix products  9.89 us (9%)
  other arithmetic  8.43 us (8%)
  starting transfers between devices  8.38 us (8%)
  waiting for transfers between devices  6.19 us (6%)
    pmax x1, blocking collectives, body(): peak_values = lax.pmax(jnp.max(series, axis=2), 'tm')  26.4 us
    psum x1, blocking collectives, body(): colsum = lax.psum(jnp.sum(normed, axis=0), 'dm')  12 us
    dot_general x3, matrix products, window_sum(): jnp.einsum('rbs,sk->rbk', paired, band_matrix, precision=lax.Precision.HI...  9.89 us
    all_gather x1, blocking collectives, body(): lax.all_gather(jnp.sum(detrended * detrended, axis=1), 'tm')  9.15 us
    unnamed x10, local copies, waits for them, and re-layouts  7.21 us
    transpose x1, local copies, waits for them, and re-layouts, boxcar(): jnp.transpose(moving, (2, 0, 1, 3))  6.85 us
    reshape x1, local copies, waits for them, and re-layouts, boxcar(): jnp.transpose(moving, (2, 0, 1, 3))  5.78 us
    reshape x1, local copies, waits for them, and re-layouts, boxcar(): moving.reshape(row_count, length // block_len, inverse.shape[0], block_len)  5.62 us
  transfers between devices with their start and end apart: 3, of which 3 were waited for; matrix products, arithmetic and copies ran while one was open for 0% of the time, Pallas kernels for 0%

profile of v1, /device:TPU:4, one launch (start us, length us, event | category | flops | bytes accessed | tf_op | source)
XLA Modules:
  0.0 108.4 jit_solution(3340712182863165493)
XLA Ops:
  0.6 1.6 %copy.23 = f32[256,1024]{0,1:T(8,128)S(1)} copy(f32[256,1024]{1,0:T(8,128)} %param.2) | data formatting | bytes 2097152 | tf_op args[0]
  2.3 1.9 %collective-permute-start = (f32[256,256]{0,1:T(8,128)S(1)}, f32[256,256]{0,1:T(8,128)S(1)}, u32[]{:S(2)}, u32[]{:S(2)}) collective-permute-start(f32[256,256]{0,1:T(8,128)S(1)} %get-tuple-element.12), channel_id=1, source_target_pairs={{0,1},{1,2},{2,3},{3,4},{4,5},{5,6},{6,7},{8,9},{9,10},{10,11},{11... | collective-permute-start | bytes 786440 | tf_op jit(solution)/shard_map/ppermute | solution.py:17
  4.2 4.5 %collective-permute-start.1 = (f32[256,256]{0,1:T(8,128)S(1)}, f32[256,256]{0,1:T(8,128)S(1)}, u32[]{:S(2)}, u32[]{:S(2)}) collective-permute-start(f32[256,256]{0,1:T(8,128)S(1)} %get-tuple-element.13), channel_id=1, source_target_pairs={{1,0},{2,1},{3,2},{4,3},{5,4},{6,5},{7,6},{9,8},{10,9},{11,10},{12... | collective-permute-start | bytes 786440 | tf_op jit(solution)/shard_map/ppermute | solution.py:18
  8.9 2.0 %collective-permute-done = f32[256,256]{0,1:T(8,128)S(1)} collective-permute-done((f32[256,256]{0,1:T(8,128)S(1)}, f32[256,256]{0,1:T(8,128)S(1)}, u32[]{:S(2)}, u32[]{:S(2)}) %collective-permute-start) | collective-permute-done | bytes 262176 | tf_op jit(solution)/shard_map/ppermute | solution.py:17
  10.9 1.7 %collective-permute-done.1 = f32[256,256]{0,1:T(8,128)S(1)} collective-permute-done((f32[256,256]{0,1:T(8,128)S(1)}, f32[256,256]{0,1:T(8,128)S(1)}, u32[]{:S(2)}, u32[]{:S(2)}) %collective-permute-start.1) | collective-permute-done | bytes 262176 | tf_op jit(solution)/shard_map/ppermute | solution.py:18
  12.7 1.3 %fusion.40 = (f32[256,5,256]{0,2,1:T(8,128)}, f32[256,5,256]{0,2,1:T(8,128)S(1)}) fusion(f32[256,6,256]{0,2,1:T(8,128)S(1)} %bitcast.23), kind=kLoop, calls=%fused_computation.58 | loop fusion | bytes 5242880 | tf_op jit(solution)/shard_map/slice | solution.py:42
  14.0 2.8 %copy.29 = f32[256,5,256]{2,0,1:T(8,128)} copy(f32[256,5,256]{0,2,1:T(8,128)} %get-tuple-element.6) | data formatting | bytes 2621440
  16.8 1.5 %copy.30 = f32[256,5,256]{2,0,1:T(8,128)} copy(f32[256,5,256]{0,2,1:T(8,128)S(1)} %get-tuple-element.7) | data formatting | bytes 2621440
  18.2 3.4 %divide_select_fusion = f32[256,5,256]{0,2,1:T(8,128)S(1)} fusion(f32[256,5,256]{2,0,1:T(8,128)} %copy.30, f32[256,5,256]{2,0,1:T(8,128)} %copy.29, f32[5,256]{1,0:T(8,128)S(1)} %add_convert_fusion, pred[5,256]{1,0:T(8,128)(4,1)S(1)} %fusion.31, s32[256]{0:T(256)S(1)} %get-tuple-element.15, s32[256]{0:T(256)S(1)} %get-tuple-element.14), kind=kOutput, calls=%fused_computation.20 | convolution fusion | flops 2014969856 | bytes 3940608 | tf_op jit(solution)/shard_map/rbs,sk->rbk/dot_general | solution.py:43
  21.8 1.3 %fusion.4 = f32[256,4,256]{0,2,1:T(8,128)S(1)} fusion(f32[256,4,256]{0,2,1:T(8,128)S(1)} %get-tuple-element.11, f32[256,4,256]{0,2,1:T(8,128)S(1)} %get-tuple-element.10, s32[256]{0:T(256)S(1)} %get-tuple-element.15, s32[256]{0:T(256)S(1)} %get-tuple-element.14), kind=kOutput, calls=%fused_computation.6 | convolution fusion | flops 1611530240 | bytes 3147776 | tf_op jit(solution)/shard_map/rbs,sk->rbk/dot_general | solution.py:43
  23.4 9.1 %all-gather.1 = f32[8,1,256]{2,1,0:T(1,128)S(1)} all-gather(f32[1,1,256]{2,1,0:T(1,128)S(1)} %bitcast.26), channel_id=2, replica_groups=mesh['dm'=4,'tm'=8] {'tm'}, dimensions={0}, use_global_device_ids=true | all-gather | bytes 9216 | tf_op jit(solution)/shard_map/all_gather | solution.py:83
  32.8 12.0 %psum.7 = f32[1024]{0:T(1024)S(1)} all-reduce(f32[1024]{0:T(1024)S(1)} %fusion.22), channel_id=1, replica_groups=mesh['dm'=4,'tm'=8] {'dm'}, use_global_device_ids=true, to_apply=%region_3.4 | all-reduce | flops 1024 | bytes 8192 | tf_op jit(solution)/shard_map/psum | solution.py:86
  45.0 1.9 %collective-permute-start.2 = (f32[256,128]{0,1:T(8,128)S(1)}, f32[256,128]{0,1:T(8,128)S(1)}, u32[]{:S(2)}, u32[]{:S(2)}) collective-permute-start(f32[256,128]{0,1:T(8,128)S(1)} %slice.42), channel_id=1, source_target_pairs={{1,0},{2,1},{3,2},{4,3},{5,4},{6,5},{7,6},{9,8},{10,9},{11,10},{12... | collective-permute-start | bytes 393224 | tf_op jit(solution)/shard_map/ppermute | solution.py:26
  47.0 2.5 %collective-permute-done.2 = f32[256,128]{0,1:T(8,128)S(1)} collective-permute-done((f32[256,128]{0,1:T(8,128)S(1)}, f32[256,128]{0,1:T(8,128)S(1)}, u32[]{:S(2)}, u32[]{:S(2)}) %collective-permute-start.2) | collective-permute-done | bytes 131104 | tf_op jit(solution)/shard_map/ppermute | solution.py:26
  49.9 0.3 copy.31
  50.2 0.3 copy.32
  50.5 5.2 %fusion.8 = f32[256,4,1024]{2,0,1:T(8,128)} fusion(f32[256,4,256]{2,0,1:T(8,128)S(1)} %copy.32, f32[256,4,256]{2,0,1:T(8,128)S(1)} %copy.31, s32[1024]{0:T(1024)S(1)} %get-tuple-element.17, s32[1024]{0:T(1024)S(1)} %get-tuple-element.16), kind=kOutput, calls=%fused_computation.10 | convolution fusion | flops 6444548096 | bytes 6299648 | tf_op jit(solution)/shard_map/rbs,sk->rbk/dot_general | solution.py:43
  55.7 5.6 %reshape.99 = f32[256,4,4,256]{3,2,0,1:T(4,128)} reshape(f32[256,4,1024]{2,0,1:T(8,128)} %fusion.8) | data formatting | bytes 8388608 | tf_op jit(solution)/shard_map/reshape | solution.py:49
  61.4 3.2 %multiply_reduce_fusion = f32[4,256]{0,1:T(8,128)S(1)} fusion(f32[4]{0:T(128)S(1)} %convert_rsqrt_fusion, f32[256,4,4,256]{3,2,0,1:T(4,128)} %reshape.99), kind=kLoop, calls=%fused_computation | loop fusion | flops 2096128 | bytes 4198416 | tf_op jit(solution)/shard_map/reduce_max | solution.py:92
  64.6 26.4 %pmax.7 = f32[4,256]{0,1:T(8,128)S(1)} all-reduce(f32[4,256]{0,1:T(8,128)S(1)} %multiply_reduce_fusion), channel_id=1, replica_groups=mesh['dm'=4,'tm'=8] {'tm'}, use_global_device_ids=true, to_apply=%region_5.6 | all-reduce | flops 1024 | bytes 8192 | tf_op jit(solution)/shard_map/pmax | solution.py:92
  90.9 0.7 copy.27
  91.6 6.9 %copy.26 = f32[4,256,4,256]{3,2,1,0:T(4,128)} copy(f32[4,256,4,256]{3,0,1,2:T(4,128)} %bitcast.22) | data formatting | bytes 8388608 | tf_op jit(solution)/shard_map/transpose | solution.py:50
  98.5 5.8 %reshape.100 = f32[4,256,1024]{2,1,0:T(8,128)} reshape(f32[4,256,4,256]{3,2,1,0:T(4,128)} %copy.26) | data formatting | bytes 8388608 | tf_op jit(solution)/shard_map/reshape | solution.py:50
  104.2 4.1 %multiply_convert_fusion = bf16[4,256,1024]{2,1,0:T(8,128)(2,1)} fusion(f32[4,256,1024]{2,1,0:T(8,128)} %reshape.100, f32[4]{0:T(128)S(1)} %convert_rsqrt_fusion), kind=kLoop, calls=%fused_computation.1 | loop fusion | flops 2097152 | bytes 6291472 | tf_op jit(solution)/shard_map/convert_element_type | solution.py:93
  (24 shorter events, 1.6 us)
Async XLA Ops:
  0.6 8.2 %copy-start = (s32[4]{0:T(128)S(1)}, s32[4]{0:T(128)}, u32[]{:S(2)}) copy-start(s32[4]{0:T(128)} %param.3) | copy-start | bytes 52
  2.3 8.7 %collective-permute-start = (f32[256,256]{0,1:T(8,128)S(1)}, f32[256,256]{0,1:T(8,128)S(1)}, u32[]{:S(2)}, u32[]{:S(2)}) collective-permute-start(f32[256,256]{0,1:T(8,128)S(1)} %get-tuple-element.12), channel_id=1, source_target_pairs={{0,1},{1,2},{2,3},{3,4},{4,5},{5,6},{6,7},{8,9},{9,10},{10,11},{11... | collective-permute-start | bytes 786440 | tf_op jit(solution)/shard_map/ppermute | solution.py:17
  4.2 8.4 %collective-permute-start.1 = (f32[256,256]{0,1:T(8,128)S(1)}, f32[256,256]{0,1:T(8,128)S(1)}, u32[]{:S(2)}, u32[]{:S(2)}) collective-permute-start(f32[256,256]{0,1:T(8,128)S(1)} %get-tuple-element.13), channel_id=1, source_target_pairs={{1,0},{2,1},{3,2},{4,3},{5,4},{6,5},{7,6},{9,8},{10,9},{11,10},{12... | collective-permute-start | bytes 786440 | tf_op jit(solution)/shard_map/ppermute | solution.py:18
  45.0 4.4 %collective-permute-start.2 = (f32[256,128]{0,1:T(8,128)S(1)}, f32[256,128]{0,1:T(8,128)S(1)}, u32[]{:S(2)}, u32[]{:S(2)}) collective-permute-start(f32[256,128]{0,1:T(8,128)S(1)} %slice.42), channel_id=1, source_target_pairs={{1,0},{2,1},{3,2},{4,3},{5,4},{6,5},{7,6},{9,8},{10,9},{11,10},{12... | collective-permute-start | bytes 393224 | tf_op jit(solution)/shard_map/ppermute | solution.py:26
